TPU v7x, 32 devices: a whole 2x2x4 slice. The times are simulated.
32 devices in a mesh: bin: 4 (over y, core), tile: 8 (over z, x).
Axes of the slice: x: 2, y: 2, z: 4, core: 2. Of those that a mesh axis runs over, the one named last changes fastest.
Arguments:
- shear_one: float32 [4, 4096, 4096], P('bin', 'tile'), may hold values from -6 to 6
- shear_two: float32 [4, 4096, 4096], P('bin', 'tile'), may hold values from -6 to 6
- weights: float32 [4, 4], replicated, may hold values from 0.2 to 1
Outputs:
- convergence: float32 [4, 4096, 4096], P('bin', 'tile')
All inputs are finite; a program needn't handle non-finite values.
Results may differ from a plain program's by a relative error of at most 0.000071.
Values sent between devices are 32-bit elements; how exact they have to be, the bound alone decides.
No kernel may reach another device: no remote copies, remote signals or barrier semaphores. Data moves between devices by JAX's collectives and lax.ppermute only.
A program may use at most 128 MiB of HBM per device.

v0:
```python
import math

import jax
import jax.numpy as jnp
from jax import lax
from jax.sharding import PartitionSpec as P


def factor_pair(length):
    leading = 1
    factor = 1
    while factor * factor <= length:
        if length % factor == 0:
            leading = factor
        factor = factor + 1
    return (leading, length // leading)


def phase_table(height, columns, modulus, orient):
    product = (
        jnp.arange(height, dtype=jnp.int32)[:, None]
        * jnp.arange(columns, dtype=jnp.int32)[None, :]
        % modulus
    )
    angles = orient * 2.0 * math.pi / modulus * product.astype(jnp.float32)
    return (jnp.cos(angles), jnp.sin(angles))


def complex_einsum(form, left_real, left_imag, right_real, right_imag):
    exact = lax.Precision.HIGHEST
    out_real = jnp.einsum(form, left_real, right_real, precision=exact) - jnp.einsum(
        form, left_imag, right_imag, precision=exact
    )
    out_imag = jnp.einsum(form, left_real, right_imag, precision=exact) + jnp.einsum(
        form, left_imag, right_real, precision=exact
    )
    return (out_real, out_imag)


def transform_last(real_part, imag_part, orient, flipped):
    batch, height, length = real_part.shape
    leading, trailing = factor_pair(length)
    outer_real, outer_imag = phase_table(leading, leading, leading, orient)
    twist_real, twist_imag = phase_table(leading, trailing, length, orient)
    inner_real, inner_imag = phase_table(trailing, trailing, trailing, orient)
    split_real = real_part.reshape(batch, height, leading, trailing)
    split_imag = imag_part.reshape(batch, height, leading, trailing)
    section_real, section_imag = complex_einsum(
        "kp,bmpq->bmkq", outer_real, outer_imag, split_real, split_imag
    )
    section_real, section_imag = (
        section_real * twist_real - section_imag * twist_imag,
        section_real * twist_imag + section_imag * twist_real,
    )
    if flipped:
        out_real, out_imag = complex_einsum(
            "bmkq,ql->blkm", section_real, section_imag, inner_real, inner_imag
        )
        return (out_real.reshape(batch, length, height), out_imag.reshape(batch, length, height))
    out_real, out_imag = complex_einsum(
        "bmkq,ql->bmlk", section_real, section_imag, inner_real, inner_imag
    )
    return (out_real.reshape(batch, height, length), out_imag.reshape(batch, height, length))


def transform_first_real(real_part, imag_part, orient):
    batch, length, height = real_part.shape
    leading, trailing = factor_pair(length)
    outer_real, outer_imag = phase_table(leading, leading, leading, orient)
    twist_real, twist_imag = phase_table(leading, trailing, length, orient)
    inner_real, inner_imag = phase_table(trailing, trailing, trailing, orient)
    split_real = real_part.reshape(batch, leading, trailing, height)
    split_imag = imag_part.reshape(batch, leading, trailing, height)
    section_real, section_imag = complex_einsum(
        "kp,bpqm->bkqm", outer_real, outer_imag, split_real, split_imag
    )
    twist_real = twist_real[:, :, None]
    twist_imag = twist_imag[:, :, None]
    section_real, section_imag = (
        section_real * twist_real - section_imag * twist_imag,
        section_real * twist_imag + section_imag * twist_real,
    )
    exact = lax.Precision.HIGHEST
    out_real = jnp.einsum("bkqm,ql->bmlk", section_real, inner_real, precision=exact) - jnp.einsum(
        "bkqm,ql->bmlk", section_imag, inner_imag, precision=exact
    )
    return out_real.reshape(batch, height, length)


def signed_frequency(index, length):
    return jnp.where(index < length // 2, index, index - length)


def apply_kernel(real_part, imag_part, column_start, length):
    block_len = real_part.shape[-2]
    col_freq = signed_frequency(column_start + jnp.arange(block_len, dtype=jnp.int32), length)[
        :, None
    ]
    row_freq = signed_frequency(jnp.arange(length, dtype=jnp.int32), length)[None, :]
    radius = col_freq * col_freq + row_freq * row_freq
    radius_floor = jnp.maximum(radius, 1).astype(jnp.float32)
    kern_real = (col_freq * col_freq - row_freq * row_freq).astype(jnp.float32) / radius_floor
    kern_imag = (2 * col_freq * row_freq).astype(jnp.float32) / radius_floor
    return (
        kern_real * real_part + kern_imag * imag_part,
        kern_real * imag_part - kern_imag * real_part,
    )


def to_space(back_real, back_imag, length):
    return transform_first_real(back_real, back_imag, 1.0) / float(length * length)


def on_device(shear_one, shear_two, weights):
    bin_count = shear_one.shape[0]
    length = shear_one.shape[2]
    total_bins = weights.shape[0]
    bin_index = lax.axis_index("bin")
    tile_index = lax.axis_index("tile")
    tile_size = lax.axis_size("tile")
    order_index = jnp.arange(total_bins, dtype=jnp.int32)
    masked = jnp.where(
        order_index[:, None] >= order_index[None, :], weights, jnp.zeros_like(weights)
    )
    row_real, row_imag = transform_last(shear_one, shear_two, -1.0, True)
    bin_size = lax.axis_size("bin")
    narrow = length // (bin_size * tile_size)
    column_start = (bin_index * tile_size + tile_index) * narrow
    mixed_real, mixed_imag = (
        lax.all_to_all(row_real, ("bin", "tile"), split_axis=1, concat_axis=2, tiled=True),
        lax.all_to_all(row_imag, ("bin", "tile"), split_axis=1, concat_axis=2, tiled=True),
    )

    def regroup(array):
        return (
            array.reshape(bin_count, narrow, bin_size, length)
            .transpose(2, 0, 1, 3)
            .reshape(total_bins, narrow, length)
        )

    def ungroup(array):
        return (
            array.reshape(bin_size, bin_count, narrow, length)
            .transpose(1, 2, 0, 3)
            .reshape(bin_count, narrow, bin_size * length)
        )

    spec_real, spec_imag = transform_last(regroup(mixed_real), regroup(mixed_imag), -1.0, False)
    spec_real, spec_imag = apply_kernel(spec_real, spec_imag, column_start, length)
    exact = lax.Precision.HIGHEST
    summed_real = jnp.einsum("ji,icn->jcn", masked, spec_real, precision=exact)
    summed_imag = jnp.einsum("ji,icn->jcn", masked, spec_imag, precision=exact)
    inverse_real, inverse_imag = transform_last(summed_real, summed_imag, 1.0, False)
    back_real, back_imag = (
        lax.all_to_all(
            ungroup(inverse_real), ("bin", "tile"), split_axis=2, concat_axis=1, tiled=True
        ),
        lax.all_to_all(
            ungroup(inverse_imag), ("bin", "tile"), split_axis=2, concat_axis=1, tiled=True
        ),
    )
    return to_space(back_real, back_imag, length)


def solution(mesh):
    in_specs = (P("bin", "tile", None), P("bin", "tile", None), P())
    out_specs = P("bin", "tile", None)
    return jax.shard_map(
        on_device, mesh=mesh, in_specs=in_specs, out_specs=out_specs, check_vma=False
    )
```

profile of v0, /device:TPU:3, one launch (start us, length us, event | category | flops | bytes accessed | tf_op | source)
XLA Modules:
  0.0 1320.4 jit_solution(11135015462587859668)
XLA Ops:
  0.0 0.1 multiply_sine_fusion.1
  0.1 9.0 copy.169
  9.1 17.9 %fusion.70 = f32[64,512,64]{1,0,2:T(8,128)} fusion(f32[512,64,64]{0,2,1:T(8,128)} %bitcast.284), kind=kOutput, calls=%fused_computation.97 | convolution fusion | flops 1610670080 | bytes 16777216 | tf_op jit(solution)/shard_map/kp,bmpq->bmkq/dot_general | solution.py:34
  27.0 13.9 %fusion.72 = f32[64,512,64]{1,0,2:T(8,128)} fusion(f32[512,64,64]{0,2,1:T(8,128)S(1)} %bitcast.285), kind=kOutput, calls=%fused_computation.99 | convolution fusion | flops 1610670080 | bytes 16777216 | tf_op jit(solution)/shard_map/kp,bmpq->bmkq/dot_general | solution.py:31
  40.8 8.9 copy.166
  49.8 17.8 %fusion.74 = f32[64,512,64]{1,0,2:T(8,128)} fusion(f32[512,64,64]{0,2,1:T(8,128)} %bitcast.288), kind=kOutput, calls=%fused_computation.101 | convolution fusion | flops 1610670080 | bytes 16777216 | tf_op jit(solution)/shard_map/kp,bmpq->bmkq/dot_general | solution.py:34
  67.6 24.8 %fusion.11 = (f32[512,64,64]{0,1,2:T(8,128)}, f32[512,64,64]{0,1,2:T(8,128)}) fusion(f32[64,64]{0,1:T(8,128)S(1)} %get-tuple-element.17, f32[64,64]{0,1:T(8,128)S(1)} %get-tuple-element.18, f32[64,512,64]{1,0,2:T(8,128)} %fusion.70, f32[64,512,64]{1,0,2:T(8,128)} %fusion.74, f32[64,512,64]{1,0,2:T(8,128)} %fusion.72, f32[512,64,64]{0,2,1:T(8,128)} %bitcast.289), kind=kOutput, calls=%fused_computation.29 | convolution fusion | flops 1627447296 | bytes 50364416 | tf_op jit(solution)/shard_map/kp,bmpq->bmkq/dot_general | solution.py:31
  92.4 17.2 %fusion.64 = f32[64,512,64]{1,0,2:T(8,128)S(1)} fusion(f32[512,64,64]{0,1,2:T(8,128)} %get-tuple-element.12), kind=kOutput, calls=%fused_computation.91 | convolution fusion | flops 1610670080 | bytes 16777216 | tf_op jit(solution)/shard_map/bmkq,ql->blkm/dot_general | solution.py:31
  109.6 12.0 subtract_bitcast_fusion.2
  121.5 5.0 copy.178
  126.6 22.8 %copy.179 = f32[1,4096,512]{2,0,1:T(1,128)} copy(f32[1,4096,512]{2,1,0:T(8,128)S(1)} %bitcast.292) | data formatting | bytes 16777216 | tf_op jit(solution)/shard_map/reshape | solution.py:59
  149.3 6.9 all-to-all-start
  156.2 16.2 %fusion.62 = f32[64,512,64]{1,0,2:T(8,128)S(1)} fusion(f32[512,64,64]{0,1,2:T(8,128)} %get-tuple-element.12), kind=kOutput, calls=%fused_computation.89 | convolution fusion | flops 1610670080 | bytes 16777216 | tf_op jit(solution)/shard_map/bmkq,ql->blkm/dot_general | solution.py:34
  172.4 17.5 %add_bitcast_fusion.2 = f32[1,64,64,512]{3,1,2,0:T(8,128)S(1)} fusion(f32[64,512,64]{1,0,2:T(8,128)S(1)} %fusion.62, f32[512,64,64]{0,1,2:T(8,128)} %get-tuple-element.11), kind=kOutput, calls=%fused_computation.47 | convolution fusion | flops 1612767232 | bytes 25165824 | tf_op jit(solution)/shard_map/bmkq,ql->blkm/dot_general | solution.py:34
  189.9 4.9 copy.185
  194.7 22.8 %copy.186 = f32[1,4096,512]{2,0,1:T(1,128)} copy(f32[1,4096,512]{2,1,0:T(8,128)S(1)} %bitcast.293) | data formatting | bytes 16777216 | tf_op jit(solution)/shard_map/reshape | solution.py:59
  217.5 125.7 %all-to-all-done = f32[1,4096,512]{2,0,1:T(1,128)} async-done(((f32[1,4096,512]{2,0,1:T(1,128)}), f32[1,4096,512]{2,0,1:T(1,128)}, u32[]{:S(2)}, u32[]{:S(2)}) %all-to-all-start) | async-done | bytes 8388640 | tf_op jit(solution)/shard_map/all_to_all | solution.py:130
  343.2 4.1 all-to-all-start.1
  347.3 0.1 multiply_sine_fusion
  347.4 2.7 convert_divide_fusion.1
  350.1 7.8 copy.269
  357.9 8.9 copy.180
  366.8 18.7 %fusion.58 = f32[4,128,64,64]{1,3,2,0:T(8,128)} fusion(f32[4,128,64,64]{1,3,2,0:T(8,128)} %bitcast.274), kind=kOutput, calls=%fused_computation.85 | convolution fusion | flops 1610670080 | bytes 16777216 | tf_op jit(solution)/shard_map/kp,bmpq->bmkq/dot_general | solution.py:34
  385.5 13.6 %fusion.60 = f32[4,128,64,64]{1,3,2,0:T(8,128)} fusion(f32[4,128,64,64]{1,3,2,0:T(8,128)S(1)} %bitcast.277), kind=kOutput, calls=%fused_computation.87 | convolution fusion | flops 1610670080 | bytes 16777216 | tf_op jit(solution)/shard_map/kp,bmpq->bmkq/dot_general | solution.py:31
  399.1 135.2 %all-to-all-done.1 = f32[1,4096,512]{2,0,1:T(1,128)} async-done(((f32[1,4096,512]{2,0,1:T(1,128)}), f32[1,4096,512]{2,0,1:T(1,128)}, u32[]{:S(2)}, u32[]{:S(2)}) %all-to-all-start.1) | async-done | bytes 8388640 | tf_op jit(solution)/shard_map/all_to_all | solution.py:131
  534.2 7.6 copy.270
  541.9 9.0 copy.187
  550.8 18.1 %fusion.56 = f32[4,128,64,64]{1,3,2,0:T(8,128)} fusion(f32[4,128,64,64]{1,3,2,0:T(8,128)} %bitcast.278), kind=kOutput, calls=%fused_computation.83 | convolution fusion | flops 1610670080 | bytes 16777216 | tf_op jit(solution)/shard_map/kp,bmpq->bmkq/dot_general | solution.py:31
  568.9 26.6 %fusion.8 = (f32[4,128,64,64]{1,2,3,0:T(8,128)}, f32[4,128,64,64]{1,2,3,0:T(8,128)}) fusion(f32[64,64]{0,1:T(8,128)S(1)} %get-tuple-element.17, f32[64,64]{0,1:T(8,128)S(1)} %get-tuple-element.18, f32[4,128,64,64]{1,3,2,0:T(8,128)} %fusion.58, f32[4,128,64,64]{1,3,2,0:T(8,128)} %fusion.60, f32[4,128,64,64]{1,3,2,0:T(8,128)} %fusion.56, ...), kind=kOutput, calls=%fused_computation.22 | convolution fusion | flops 1627447296 | bytes 50364416 | tf_op jit(solution)/shard_map/kp,bmpq->bmkq/dot_general | solution.py:34
  595.5 18.7 %fusion.48 = f32[64,4,128,64]{2,0,3,1:T(8,128)} fusion(f32[4,128,64,64]{1,2,3,0:T(8,128)} %get-tuple-element.10), kind=kOutput, calls=%fused_computation.75 | convolution fusion | flops 1610670080 | bytes 16777216 | tf_op jit(solution)/shard_map/bmkq,ql->bmlk/dot_general | solution.py:31
  614.3 0.0 slice-start.3
  614.3 12.6 fusion.46
  627.0 15.8 %subtract_bitcast_fusion.1 = f32[4,128,64,64]{1,2,3,0:T(8,128)} fusion(f32[64,4,128,64]{2,0,3,1:T(8,128)} %fusion.48, f32[4,128,64,64]{1,2,3,0:T(8,128)S(1)} %bitcast.281), kind=kOutput, calls=%fused_computation.46 | convolution fusion | flops 1612767232 | bytes 25165824 | tf_op jit(solution)/shard_map/bmkq,ql->bmlk/dot_general | solution.py:31
  642.7 11.5 copy.196
  654.2 13.6 %add_bitcast_fusion.1 = f32[4,128,64,64]{1,2,3,0:T(8,128)} fusion(f32[64,4,128,64]{2,0,3,1:T(8,128)S(1)} %fusion.46, f32[4,128,64,64]{1,2,3,0:T(8,128)S(1)} %bitcast.281), kind=kOutput, calls=%fused_computation.45 | convolution fusion | flops 1612767232 | bytes 25165824 | tf_op jit(solution)/shard_map/bmkq,ql->bmlk/dot_general | solution.py:34
  667.8 11.7 copy.199
  679.5 9.1 fusion.6
  688.5 25.0 %fusion.20 = f32[4,128,64,64]{1,0,3,2:T(4,128)S(1)} fusion(f32[128,64,64,4]{0,2,1,3:T(8,128)} %bitcast.300, f32[4,4]{1,0:T(4,128)S(1)} %copy-done.9), kind=kOutput, calls=%fused_computation.40 | convolution fusion | flops 100663328 | bytes 16777280 | tf_op jit(solution)/shard_map/ji,icn->jcn/dot_general | solution.py:151
  713.5 0.0 slice-start.4
  713.6 13.8 %fusion.42 = f32[4,128,64,64]{1,3,2,0:T(8,128)} fusion(f32[4,128,64,64]{1,0,3,2:T(4,128)S(1)} %fusion.20), kind=kOutput, calls=%fused_computation.69 | convolution fusion | flops 1610670080 | bytes 16777216 | tf_op jit(solution)/shard_map/kp,bmpq->bmkq/dot_general | solution.py:34
  727.4 13.3 %fusion.44 = f32[4,128,64,64]{1,3,2,0:T(8,128)} fusion(f32[4,128,64,64]{1,0,3,2:T(4,128)S(1)} %fusion.20), kind=kOutput, calls=%fused_computation.71 | convolution fusion | flops 1610670080 | bytes 16777216 | tf_op jit(solution)/shard_map/kp,bmpq->bmkq/dot_general | solution.py:31
  740.7 18.3 %fusion.18 = f32[4,128,64,64]{1,0,3,2:T(4,128)S(1)} fusion(f32[128,64,64,4]{0,2,1,3:T(8,128)S(1)} %bitcast.299, f32[4,4]{1,0:T(4,128)S(1)} %copy-done.9), kind=kOutput, calls=%fused_computation.38 | convolution fusion | flops 100663328 | bytes 16777280 | tf_op jit(solution)/shard_map/ji,icn->jcn/dot_general | solution.py:152
  759.1 13.5 %fusion.40 = f32[4,128,64,64]{1,3,2,0:T(8,128)} fusion(f32[4,128,64,64]{1,0,3,2:T(4,128)S(1)} %fusion.18), kind=kOutput, calls=%fused_computation.67 | convolution fusion | flops 1610670080 | bytes 16777216 | tf_op jit(solution)/shard_map/kp,bmpq->bmkq/dot_general | solution.py:31
  772.5 26.6 %fusion.4 = (f32[4,128,64,64]{1,2,3,0:T(8,128)}, f32[4,128,64,64]{1,2,3,0:T(8,128)}) fusion(f32[64,64]{0,1:T(8,128)S(1)} %get-tuple-element.23, f32[64,64]{0,1:T(8,128)S(1)} %get-tuple-element.24, f32[4,128,64,64]{1,3,2,0:T(8,128)} %fusion.42, f32[4,128,64,64]{1,3,2,0:T(8,128)} %fusion.44, f32[4,128,64,64]{1,3,2,0:T(8,128)} %fusion.40, ...), kind=kOutput, calls=%fused_computation.10 | convolution fusion | flops 1627447296 | bytes 50364416 | tf_op jit(solution)/shard_map/kp,bmpq->bmkq/dot_general | solution.py:34
  799.1 15.8 %fusion.30 = f32[64,4,128,64]{2,0,3,1:T(8,128)S(1)} fusion(f32[4,128,64,64]{1,2,3,0:T(8,128)} %get-tuple-element.8), kind=kOutput, calls=%fused_computation.57 | convolution fusion | flops 1610670080 | bytes 16777216 | tf_op jit(solution)/shard_map/bmkq,ql->bmlk/dot_general | solution.py:34
  814.9 12.0 add_bitcast_fusion
  827.0 8.4 copy.219
  835.3 3.7 all-to-all-start.3
  839.0 15.5 %fusion.32 = f32[64,4,128,64]{2,0,3,1:T(8,128)S(1)} fusion(f32[4,128,64,64]{1,2,3,0:T(8,128)} %get-tuple-element.8), kind=kOutput, calls=%fused_computation.59 | convolution fusion | flops 1610670080 | bytes 16777216 | tf_op jit(solution)/shard_map/bmkq,ql->bmlk/dot_general | solution.py:31
  854.5 16.0 %subtract_bitcast_fusion = f32[4,128,64,64]{1,2,3,0:T(8,128)S(1)} fusion(f32[64,4,128,64]{2,0,3,1:T(8,128)S(1)} %fusion.32, f32[4,128,64,64]{1,2,3,0:T(8,128)} %get-tuple-element.7), kind=kOutput, calls=%fused_computation.44 | convolution fusion | flops 1612767232 | bytes 25165824 | tf_op jit(solution)/shard_map/bmkq,ql->bmlk/dot_general | solution.py:31
  870.5 8.1 copy.212
  878.6 147.6 %all-to-all-done.3 = f32[1,128,16384]{1,0,2:T(1,128)} async-done(((f32[1,128,16384]{1,0,2:T(1,128)}), f32[1,128,16384]{1,0,2:T(1,128)}, u32[]{:S(2)}, u32[]{:S(2)}) %all-to-all-start.3) | async-done | bytes 8388640 | tf_op jit(solution)/shard_map/all_to_all | solution.py:158
  1026.2 4.1 all-to-all-start.2
  1030.3 9.0 copy.221
  1039.2 18.1 %fusion.22 = f32[64,512,64]{1,2,0:T(8,128)} fusion(f32[64,64,512]{2,1,0:T(8,128)} %bitcast.282), kind=kOutput, calls=%fused_computation.49 | convolution fusion | flops 1610670080 | bytes 16777216 | tf_op jit(solution)/shard_map/kp,bpqm->bkqm/dot_general | solution.py:34
  1057.3 13.8 %fusion.24 = f32[64,512,64]{1,2,0:T(8,128)} fusion(f32[64,64,512]{2,1,0:T(8,128)S(1)} %bitcast.283), kind=kOutput, calls=%fused_computation.51 | convolution fusion | flops 1610670080 | bytes 16777216 | tf_op jit(solution)/shard_map/kp,bpqm->bkqm/dot_general | solution.py:31
  1071.1 146.1 %all-to-all-done.2 = f32[1,128,16384]{1,0,2:T(1,128)} async-done(((f32[1,128,16384]{1,0,2:T(1,128)}), f32[1,128,16384]{1,0,2:T(1,128)}, u32[]{:S(2)}, u32[]{:S(2)}) %all-to-all-start.2) | async-done | bytes 8388640 | tf_op jit(solution)/shard_map/all_to_all | solution.py:155
  1217.2 8.9 copy.214
  1226.2 18.1 %fusion.26 = f32[64,512,64]{1,2,0:T(8,128)} fusion(f32[64,64,512]{2,1,0:T(8,128)} %bitcast.286), kind=kOutput, calls=%fused_computation.53 | convolution fusion | flops 1610670080 | bytes 16777216 | tf_op jit(solution)/shard_map/kp,bpqm->bkqm/dot_general | solution.py:34
  1244.2 29.2 %fusion.1 = (f32[64,64,512]{2,0,1:T(8,128)}, f32[64,64,512]{2,0,1:T(8,128)}) fusion(f32[64,64]{0,1:T(8,128)S(1)} %get-tuple-element.23, f32[64,64]{0,1:T(8,128)S(1)} %get-tuple-element.24, f32[64,512,64]{1,2,0:T(8,128)} %fusion.22, f32[64,512,64]{1,2,0:T(8,128)} %fusion.26, f32[64,512,64]{1,2,0:T(8,128)} %fusion.24, f32[64,64,512]{2,1,0:T(8,128)} %bitcast.287), kind=kOutput, calls=%fused_computation.3 | convolution fusion | flops 1627447296 | bytes 50364416 | tf_op jit(solution)/shard_map/kp,bpqm->bkqm/dot_general | solution.py:31
  1273.4 16.9 %fusion.14 = f32[64,64,512]{2,0,1:T(8,128)S(1)} fusion(f32[64,64,512]{2,0,1:T(8,128)} %get-tuple-element.6), kind=kOutput, calls=%fused_computation.34 | convolution fusion | flops 1610670080 | bytes 16777216 | tf_op jit(solution)/shard_map/bkqm,ql->bmlk/dot_general | solution.py:84
  1290.3 12.7 multiply_bitcast_fusion
  1303.1 8.1 copy.230
  1311.2 8.9 copy.231
  (35 shorter events, 0.1 us)
Async XLA Ops:
  9.1 17.9 %copy-start.4 = (f32[1,512,4096]{1,2,0:T(8,128)S(1)}, f32[1,512,4096]{1,2,0:T(8,128)}, u32[]{:S(2)}) copy-start(f32[1,512,4096]{1,2,0:T(8,128)} %copy.169) | copy-start | bytes 25165828
  92.4 17.2 %copy-start.1 = (f32[512,64,64]{0,1,2:T(8,128)S(1)}, f32[512,64,64]{0,1,2:T(8,128)}, u32[]{:S(2)}) copy-start(f32[512,64,64]{0,1,2:T(8,128)} %get-tuple-element.11) | copy-start | bytes 25165828
  149.3 193.9 %all-to-all-start = ((f32[1,4096,512]{2,0,1:T(1,128)}), f32[1,4096,512]{2,0,1:T(1,128)}, u32[]{:S(2)}, u32[]{:S(2)}) async-start(f32[1,4096,512]{2,0,1:T(1,128)} %copy.179), calls=%async_computation | async-start | bytes 16777216 | tf_op jit(solution)/shard_map/all_to_all | solution.py:130
  343.2 191.1 %all-to-all-start.1 = ((f32[1,4096,512]{2,0,1:T(1,128)}), f32[1,4096,512]{2,0,1:T(1,128)}, u32[]{:S(2)}, u32[]{:S(2)}) async-start(f32[1,4096,512]{2,0,1:T(1,128)} %copy.186), calls=%async_computation.1 | async-start | bytes 16777216 | tf_op jit(solution)/shard_map/all_to_all | solution.py:131
  366.8 18.7 %slice-start = ((s8[8388608]{0:T(1024)(128)(4,1)}), s8[4194304]{0:T(1024)(128)(4,1)S(1)}, s32[]{:S(2)}) async-start(s8[8388608]{0:T(1024)(128)(4,1)} %bitcast.275), calls=%async_computation.4 | async-start | bytes 8388608
  366.8 18.7 %slice-start.1 = ((s8[8388608]{0:T(1024)(128)(4,1)}), s8[4194304]{0:T(1024)(128)(4,1)S(1)}, s32[]{:S(2)}) async-start(s8[8388608]{0:T(1024)(128)(4,1)} %bitcast.275), calls=%async_computation.5 | async-start | bytes 8388608
  595.5 18.8 %copy-start.5 = (f32[4,128,64,64]{1,2,3,0:T(8,128)S(1)}, f32[4,128,64,64]{1,2,3,0:T(8,128)}, u32[]{:S(2)}) copy-start(f32[4,128,64,64]{1,2,3,0:T(8,128)} %get-tuple-element.10) | copy-start | bytes 25165828
  595.5 31.4 %slice-start.2 = ((s8[8388608]{0:T(1024)(128)(4,1)}), s8[4194304]{0:T(1024)(128)(4,1)S(1)}, s32[]{:S(2)}) async-start(s8[8388608]{0:T(1024)(128)(4,1)} %bitcast.280), calls=%async_computation.6 | async-start | bytes 8388608
  614.3 12.6 slice-start.3
  667.8 11.7 copy-start.7
  667.8 11.7 copy-start.8
  679.5 9.1 copy-start.9
  713.5 27.2 %slice-start.4 = ((s8[8388608]{0:T(1024)(128)(4,1)}), s8[4194304]{0:T(1024)(128)(4,1)S(1)}, s32[]{:S(2)}) async-start(s8[8388608]{0:T(1024)(128)(4,1)} %bitcast.297), calls=%async_computation.8 | async-start | bytes 8388608
  727.4 13.3 %slice-start.5 = ((s8[8388608]{0:T(1024)(128)(4,1)}), s8[4194304]{0:T(1024)(128)(4,1)S(1)}, s32[]{:S(2)}) async-start(s8[8388608]{0:T(1024)(128)(4,1)} %bitcast.297), calls=%async_computation.9 | async-start | bytes 8388608
  759.0 13.5 %copy-start = (f32[4,128,64,64]{1,0,3,2:T(4,128)}, f32[4,128,64,64]{1,0,3,2:T(4,128)S(1)}, u32[]{:S(2)}) copy-start(f32[4,128,64,64]{1,0,3,2:T(4,128)S(1)} %fusion.18) | copy-start | bytes 25165828
  799.1 15.9 %copy-start.2 = (f32[4,128,64,64]{1,2,3,0:T(8,128)S(1)}, f32[4,128,64,64]{1,2,3,0:T(8,128)}, u32[]{:S(2)}) copy-start(f32[4,128,64,64]{1,2,3,0:T(8,128)} %get-tuple-element.7) | copy-start | bytes 25165828
  835.3 190.9 %all-to-all-start.3 = ((f32[1,128,16384]{1,0,2:T(1,128)}), f32[1,128,16384]{1,0,2:T(1,128)}, u32[]{:S(2)}, u32[]{:S(2)}) async-start(f32[1,128,16384]{1,0,2:T(1,128)} %bitcast.291), calls=%async_computation.3 | async-start | bytes 16777216 | tf_op jit(solution)/shard_map/all_to_all | solution.py:158
  1026.2 191.1 %all-to-all-start.2 = ((f32[1,128,16384]{1,0,2:T(1,128)}), f32[1,128,16384]{1,0,2:T(1,128)}, u32[]{:S(2)}, u32[]{:S(2)}) async-start(f32[1,128,16384]{1,0,2:T(1,128)} %bitcast.290), calls=%async_computation.2 | async-start | bytes 16777216 | tf_op jit(solution)/shard_map/all_to_all | solution.py:155
  1039.2 18.1 %copy-start.3 = (f32[1,32,128,512]{3,2,1,0:T(8,128)S(1)}, f32[1,32,128,512]{3,2,1,0:T(8,128)}, u32[]{:S(2)}) copy-start(f32[1,32,128,512]{3,2,1,0:T(8,128)} %copy.221) | copy-start | bytes 25165828
  1273.4 16.9 %copy-start.6 = (f32[64,64,512]{2,0,1:T(8,128)S(1)}, f32[64,64,512]{2,0,1:T(8,128)}, u32[]{:S(2)}) copy-start(f32[64,64,512]{2,0,1:T(8,128)} %get-tuple-element.5) | copy-start | bytes 25165828
where the time goes:
time: 1330 us; the launch traced here: 1320 us
  waiting for transfers between devices  555 us (42%)
  matrix products  553 us (42%)
  local copies, waits for them, and re-layouts  181 us (14%)
  starting transfers between devices  18.7 us (1%)
    all_to_all x1, waiting for transfers between devices, on_device(): lax.all_to_all(ungroup(inverse_imag), ('bin', 'tile'), split_axis=2, conc...  148 us
    all_to_all x1, waiting for transfers between devices, on_device(): lax.all_to_all(ungroup(inverse_real), ('bin', 'tile'), split_axis=2, conc...  146 us
    all_to_all x1, waiting for transfers between devices, on_device(): lax.all_to_all(row_imag, ('bin', 'tile'), split_axis=1, concat_axis=2, ti...  135 us
    dot_general x7, matrix products, complex_einsum(): jnp.einsum(form, left_real, right_imag, precision=exact)  132 us
    all_to_all x1, waiting for transfers between devices, on_device(): lax.all_to_all(row_real, ('bin', 'tile'), split_axis=1, concat_axis=2, ti...  126 us
    dot_general x7, matrix products, complex_einsum(): jnp.einsum(form, left_real, right_real, precision=exact)  124 us
    dot_general x7, matrix products, complex_einsum(): jnp.einsum(form, left_imag, right_real, precision=exact)  113 us
    dot_general x7, matrix products, complex_einsum(): jnp.einsum(form, left_imag, right_imag, precision=exact)  111 us
  transfers between devices with their start and end apart: 4, of which 4 were waited for; matrix products, arithmetic and copies ran while one was open for 15% of the time, Pallas kernels for 0%

commit v1 on v0

v1 whole, which is shorter than its diff:
```python
import functools

import jax
import jax.numpy as jnp
import ml_dtypes
import numpy as np
from jax import lax
from jax.experimental import pallas as pl
from jax.experimental.pallas import tpu as pltpu
from jax.sharding import PartitionSpec as P

LANES = 128
SUBLANES = 8
CHUNKS = 2


def complex_times(real, imag, factor):
    fr, fi = factor.real, factor.imag
    if abs(fi) < 1e-12:
        fr = round(fr) if abs(abs(fr) - 1) < 1e-12 else fr
        if fr == 1:
            return real, imag
        if fr == -1:
            return -real, None if imag is None else -imag
        return real * fr, None if imag is None else imag * fr
    if abs(fr) < 1e-12:
        sign = 1 if fi > 0 else -1
        if imag is None:
            return None, real if sign > 0 else -real
        return (-imag, real) if sign > 0 else (imag, -real)
    if imag is None:
        return real * fr, real * fi
    if abs(abs(fr) - abs(fi)) < 1e-12:
        size, sr, si = abs(fr), fr > 0, fi > 0
        re = (real - imag) if sr == si else (real + imag)
        im = (real + imag) if sr == si else (imag - real)
        if sr and si:
            return re * size, im * size
        if not sr and not si:
            return re * -size, im * -size
        if sr:
            return re * size, im * size
        return re * -size, im * -size
    return real * fr - imag * fi, real * fi + imag * fr


def plus(a, b):
    return b if a is None else a if b is None else a + b


def minus(a, b):
    return a if b is None else -b if a is None else a - b


def full_transform(values, orient):
    size = len(values)
    if size == 1:
        return values
    even = full_transform(values[0::2], orient)
    odd = full_transform(values[1::2], orient)
    half = size // 2
    out = [None] * size
    for k in range(half):
        tr, ti = complex_times(*odd[k], np.exp(orient * 2j * np.pi * k / size))
        er, ei = even[k]
        out[k] = (plus(er, tr), plus(ei, ti))
        out[k + half] = (minus(er, tr), minus(ei, ti))
    return out


def real_transform(values):
    size = len(values)
    if size == 2:
        return [(values[0] + values[1], None), (values[0] - values[1], None)]
    even = real_transform(values[0::2])
    odd = real_transform(values[1::2])
    half = size // 2
    out = [None] * (half + 1)
    for k in range(size // 4 + 1):
        tr, ti = complex_times(*odd[k], np.exp(-2j * np.pi * k / size))
        er, ei = even[k]
        low = minus(ei, ti)
        out[half - k] = (minus(er, tr), None if low is None else -low)
        out[k] = (plus(er, tr), plus(ei, ti))
    return out


def real_inverse(spectrum):
    size = 2 * (len(spectrum) - 1)
    if size == 2:
        return [spectrum[0][0] + spectrum[1][0], spectrum[0][0] - spectrum[1][0]]
    half = size // 2
    even, odd = [], []
    for k in range(size // 4 + 1):
        ar, ai = spectrum[k]
        br, bi = spectrum[half - k]
        if k == size // 4:
            even.append((ar + ar, None))
            odd.append((-(ai + ai), None))
            continue
        er, ei = plus(ar, br), minus(ai, bi)
        dr, di = minus(ar, br), plus(ai, bi)
        if k == 0:
            ei = di = None
        even.append((er, ei))
        odd.append(complex_times(dr, di, np.exp(2j * np.pi * k / size)))
    out = [None] * size
    out[0::2] = real_inverse(even)
    out[1::2] = real_inverse(odd)
    return out


def halves(matrix):
    high = matrix.astype(ml_dtypes.bfloat16)
    low = (matrix - high.astype(np.float64)).astype(ml_dtypes.bfloat16)
    return np.stack([high, low])


def column_places(narrow, chunks):
    wide = narrow // chunks
    chunk, holder, part, column = np.meshgrid(
        np.arange(chunks), np.arange(LANES // narrow), np.arange(2), np.arange(wide), indexing="ij"
    )
    return part.reshape(-1), (holder * narrow + chunk * wide + column).reshape(-1)


def lane_transform(orient):
    index = np.arange(LANES)
    angle = orient * 2 * np.pi * np.outer(index, index) / LANES
    cos, sin = np.cos(angle), np.sin(angle)
    return np.block([[cos, sin], [-sin, cos]])


def row_matrices(length, narrow, chunks):
    pieces = length // LANES
    part, column = column_places(narrow, chunks)
    q = np.arange(LANES)
    angle = 2 * np.pi * np.outer(column, q) / LANES
    cos, sin = np.cos(angle), np.sin(angle)
    real = (part == 0)[:, None]
    forward = np.where(real, np.hstack([cos, sin]), np.hstack([-sin, cos]))
    inverse = np.where(real, np.hstack([cos, sin]), np.hstack([-sin, cos]))
    late = (column >= LANES // 2)[:, None]
    within = np.where(column >= LANES // 2, column - LANES // 2, column)
    angle = 2 * np.pi * (np.outer(within, q) / LANES + late * (pieces // 2) * q[None, :] / length)
    wave = np.where(real, np.cos(angle), -np.sin(angle))
    first = (column == 0)[:, None]
    wave = np.where(first & ~real, 1.0 - 2.0 * (q % 2)[None, :], wave)
    zero = np.zeros_like(wave)
    edge_forward = np.where(late, np.hstack([zero, wave]), np.hstack([wave, zero]))
    edge_inverse = edge_forward * np.where(first, 1.0, 2.0)
    return halves(forward), halves(inverse), halves(edge_forward), halves(edge_inverse)


def twiddle(length):
    pieces = length // LANES
    angle = 2 * np.pi * np.outer(np.arange(pieces), np.arange(LANES)) / length
    table = np.stack([np.cos(angle), np.sin(angle)]).astype(np.float32)
    return np.ascontiguousarray(
        np.broadcast_to(table[:, :, None, :], (2, pieces, SUBLANES, LANES))
    )


def parts_of(values):
    high = values.astype(jnp.bfloat16)
    low = (values - high.astype(jnp.float32)).astype(jnp.bfloat16)
    return high, low


def product(left, right, dims):
    dot = functools.partial(
        lax.dot_general, dimension_numbers=(dims, ((), ())), preferred_element_type=jnp.float32
    )
    return dot(left[0], right[0]) + dot(left[0], right[1]) + dot(left[1], right[0])


def rows_kernel(one_ref, two_ref, matrix_ref, edge_ref, twiddle_ref, *refs):
    *out_refs, mid_ref = refs
    rows = one_ref.shape[0]
    blocks = mid_ref.shape[0]
    pieces = 2 * blocks
    chunks = len(out_refs)
    holders, wide = out_refs[0].shape[1], out_refs[0].shape[4]

    for field, ref in enumerate((one_ref, two_ref)):

        def over_pieces(step, carry, ref=ref):
            at = pl.ds(pl.multiple_of(step * SUBLANES, SUBLANES), SUBLANES)
            values = [ref[at, p * LANES : (p + 1) * LANES] for p in range(pieces)]
            spectrum = real_transform(values)
            mid_ref[0, at, :LANES] = spectrum[0][0]
            mid_ref[0, at, LANES:] = spectrum[blocks][0]
            for k in range(1, blocks):
                real, imag = spectrum[k]
                cos, sin = twiddle_ref[0, k], twiddle_ref[1, k]
                mid_ref[k, at, :LANES] = real * cos + imag * sin
                mid_ref[k, at, LANES:] = imag * cos - real * sin
            return carry

        lax.fori_loop(0, rows // SUBLANES, over_pieces, 0)

        def over_lanes(k, matrix_ref, field=field):
            result = product(
                (matrix_ref[0], matrix_ref[1]), parts_of(mid_ref[k]), (((1,), (1,)))
            )
            at = 0
            for chunk in range(chunks):
                for holder in range(holders):
                    for part in range(2):
                        out_refs[chunk][k, holder, field, part] = result[at : at + wide]
                        at += wide

        over_lanes(0, edge_ref)

        def each(k, carry, over_lanes=over_lanes):
            over_lanes(k, matrix_ref)
            return carry

        lax.fori_loop(1, blocks, each, 0)


def columns_kernel(
    flag_ref, weights_ref, in_ref, freq_ref, forward_ref, inverse_ref, twiddle_ref, out_ref, mid_ref, hat_ref, two_ref
):
    total_bins = weights_ref.shape[0]
    tiles = in_ref.shape[0] // total_bins
    span = in_ref.shape[4] // LANES
    pieces = tiles * span
    length = pieces * LANES
    special = jnp.logical_and(flag_ref[0] == 1, pl.program_id(0) == 0)
    sublane = lax.broadcasted_iota(jnp.int32, (SUBLANES, LANES), 0)
    lane = lax.broadcasted_iota(jnp.int32, (SUBLANES, LANES), 1)
    packed = jnp.logical_and(sublane == 0, special)
    col_freq = freq_ref[...]

    def factors(k, col_freq):
        index = lane * pieces + k
        row_freq = jnp.where(index < length // 2, index, index - length).astype(jnp.float32)
        col_sq, row_sq = col_freq * col_freq, row_freq * row_freq
        floor = jnp.maximum(col_sq + row_sq, 1.0)
        return (col_sq - row_sq) / floor, 2.0 * col_freq * row_freq / floor

    def store_mid(spectrum, orient):
        for k, (real, imag) in enumerate(spectrum):
            at = slice(k * SUBLANES, (k + 1) * SUBLANES)
            if k == 0:
                mid_ref[at, :LANES] = real
                mid_ref[at, LANES:] = imag
                continue
            cos, sin = twiddle_ref[0, k], twiddle_ref[1, k]
            mid_ref[at, :LANES] = real * cos + imag * sin
            mid_ref[at, LANES:] = imag * cos - real * sin

    def forward_of(bin_at, field):
        values = []
        for p in range(pieces):
            at = bin_at * tiles + p // span
            cut = slice((p % span) * LANES, (p % span + 1) * LANES)
            real = in_ref[at, field, 0, :, cut]
            imag = in_ref[at, field, 1, :, cut]
            if field == 0:
                imag = jnp.where(packed, 0.0, imag)
            else:
                real = jnp.where(packed, 0.0, real)
                imag = jnp.where(packed, in_ref[at, 0, 1, :, cut], imag)
            values.append((real, imag))
        store_mid(full_transform(values, -1), -1)
        return product(parts_of(mid_ref[...]), (forward_ref[0], forward_ref[1]), ((1,), (0,)))

    def each_bin(bin_at, carry):
        one = forward_of(bin_at, 0)
        hat_ref[bin_at] = one
        two_ref[...] = forward_of(bin_at, 1)

        for k in range(pieces):
            at = slice(k * SUBLANES, (k + 1) * SUBLANES)
            kern_real, kern_imag = factors(k, col_freq)
            one_real, one_imag = hat_ref[bin_at, at, :LANES], hat_ref[bin_at, at, LANES:]
            two_real, two_imag = two_ref[at, :LANES], two_ref[at, LANES:]
            hat_real = kern_real * one_real + kern_imag * two_real
            hat_imag = kern_real * one_imag + kern_imag * two_imag
            if k == 0:
                middle = lane == LANES // 2
                hat_real = jnp.where(middle, kern_real * one_real + kern_imag * one_imag, hat_real)
                hat_imag = jnp.where(middle, kern_real * one_imag - kern_imag * one_real, hat_imag)
            hat_ref[bin_at, at, :LANES] = hat_real
            hat_ref[bin_at, at, LANES:] = hat_imag

        @pl.when(special)
        def _():
            total = jnp.zeros((SUBLANES, LANES), jnp.float32)
            for p in range(pieces):
                cut = slice((p % span) * LANES, (p % span + 1) * LANES)
                total = total + in_ref[bin_at * tiles + p // span, 1, 1, :, cut]
            signed = jnp.where(lane % 2 == 0, total, -total)
            corner = jnp.sum(signed, axis=1, keepdims=True)
            edge_freq = jnp.full((SUBLANES, LANES), -(length // 2), jnp.float32)
            for k in range(pieces):
                at = slice(k * SUBLANES, (k + 1) * SUBLANES)
                kern_real, kern_imag = factors(k, edge_freq)
                two_real, two_imag = two_ref[at, :LANES], two_ref[at, LANES:]
                add_real = kern_real * two_real + kern_imag * two_imag
                add_imag = kern_real * two_imag - kern_imag * two_real
                if k == 0:
                    middle = lane == LANES // 2
                    add_real = jnp.where(middle, 0.0, add_real)
                    add_imag = jnp.where(middle, jnp.broadcast_to(corner, add_imag.shape), add_imag)
                hat_ref[bin_at, at, :LANES] += jnp.where(sublane == 0, add_real, 0.0)
                hat_ref[bin_at, at, LANES:] += jnp.where(sublane == 0, add_imag, 0.0)

        return carry

    lax.fori_loop(0, total_bins, each_bin, 0)

    def each_source(source, carry):
        summed = weights_ref[source, 0] * hat_ref[0]
        for bin_at in range(1, total_bins):
            summed = summed + weights_ref[source, bin_at] * hat_ref[bin_at]
        mid_ref[...] = product(parts_of(summed), (inverse_ref[0], inverse_ref[1]), ((1,), (0,)))
        values = []
        for k in range(pieces):
            at = slice(k * SUBLANES, (k + 1) * SUBLANES)
            real, imag = mid_ref[at, :LANES], mid_ref[at, LANES:]
            if k:
                cos, sin = twiddle_ref[0, k], twiddle_ref[1, k]
                real, imag = real * cos - imag * sin, imag * cos + real * sin
            values.append((real, imag))
        for p, (real, imag) in enumerate(full_transform(values, 1)):
            at = source * tiles + p // span
            cut = slice((p % span) * LANES, (p % span + 1) * LANES)
            out_ref[at, 0, :, cut] = real
            out_ref[at, 1, :, cut] = imag
        return carry

    lax.fori_loop(0, total_bins, each_source, 0)


def back_kernel(*refs):
    *in_refs, matrix_ref, edge_ref, twiddle_ref, out_ref, mid_ref = refs
    rows = out_ref.shape[0]
    blocks = mid_ref.shape[0]
    pieces = 2 * blocks
    holders = in_refs[0].shape[1]

    def over_lanes(k, matrix_ref):
        slabs = [ref[k, holder, part] for ref in in_refs for holder in range(holders) for part in range(2)]
        values = jnp.concatenate(slabs, axis=0).T
        mid_ref[k] = product(parts_of(values), (matrix_ref[0], matrix_ref[1]), ((1,), (0,)))

    over_lanes(0, edge_ref)

    def each(k, carry):
        over_lanes(k, matrix_ref)
        return carry

    lax.fori_loop(1, blocks, each, 0)

    def over_pieces(step, carry):
        at = pl.ds(pl.multiple_of(step * SUBLANES, SUBLANES), SUBLANES)
        spectrum = [(mid_ref[0, at, :LANES], None)]
        for k in range(1, blocks):
            real, imag = mid_ref[k, at, :LANES], mid_ref[k, at, LANES:]
            cos, sin = twiddle_ref[0, k], twiddle_ref[1, k]
            spectrum.append((real * cos - imag * sin, imag * cos + real * sin))
        spectrum.append((mid_ref[0, at, LANES:], None))
        for p, value in enumerate(real_inverse(spectrum)):
            out_ref[at, p * LANES : (p + 1) * LANES] = value
        return carry

    lax.fori_loop(0, rows // SUBLANES, over_pieces, 0)


def whole(shape):
    return pl.BlockSpec(shape, lambda i: (0,) * len(shape))


def on_device(shear_one, shear_two, weights):
    bins_here, rows, length = shear_one.shape
    total_bins = weights.shape[0]
    tiles = lax.axis_size("tile")
    holders_all = lax.axis_size("bin") * tiles
    pieces = length // LANES
    blocks = pieces // 2
    narrow = length // 2 // holders_all
    wide = narrow // CHUNKS
    holders = LANES // narrow
    assert bins_here == 1 and wide % SUBLANES == 0 and rows % LANES == 0
    step_rows = min(rows, 2 * LANES)
    limit = pltpu.CompilerParams(vmem_limit_bytes=56 * 1024 * 1024)

    forward, inverse, edge_forward, edge_inverse = row_matrices(length, narrow, CHUNKS)
    table = twiddle(length)
    order_index = jnp.arange(total_bins, dtype=jnp.int32)
    masked = jnp.where(
        order_index[:, None] >= order_index[None, :], weights, jnp.zeros_like(weights)
    )

    matrix_shape = (2, 2 * LANES, 2 * LANES)
    shear_spec = pl.BlockSpec((step_rows, length), lambda i: (i, 0))
    sent = pl.pallas_call(
        rows_kernel,
        name="rows_forward",
        grid=(rows // step_rows,),
        in_specs=[shear_spec, shear_spec, whole(matrix_shape), whole(matrix_shape), whole(table.shape)],
        out_specs=[
            pl.BlockSpec((blocks, holders, 2, 2, wide, step_rows), lambda i: (0, 0, 0, 0, 0, i))
        ] * CHUNKS,
        out_shape=[jax.ShapeDtypeStruct((blocks, holders, 2, 2, wide, rows), jnp.float32)] * CHUNKS,
        scratch_shapes=[pltpu.VMEM((blocks, step_rows, 2 * LANES), jnp.float32)],
        compiler_params=limit,
    )(shear_one[0], shear_two[0], forward, edge_forward, table)

    device = lax.axis_index("bin") * tiles + lax.axis_index("tile")
    column = device * narrow + jnp.arange(narrow, dtype=jnp.int32)
    block, within = column // LANES, column % LANES
    edge = jnp.where(within < LANES // 2, within * pieces, (within - LANES // 2) * pieces + blocks)
    frequency = jnp.where(block == 0, edge, block + pieces * within)
    signed = jnp.where(frequency < length // 2, frequency, frequency - length)
    col_freq = jnp.broadcast_to(signed.astype(jnp.float32)[:, None], (narrow, LANES))
    first = (device == 0).astype(jnp.int32)

    to_frequency = halves(lane_transform(-1))
    to_rows = halves(lane_transform(1) / float(length) ** 2)
    returned = []
    for chunk in range(CHUNKS):
        got = lax.all_to_all(
            sent[chunk].reshape(holders_all, 2, 2, wide, rows),
            ("bin", "tile"), split_axis=0, concat_axis=0, tiled=True,
        )
        flag = jnp.reshape(first if chunk == 0 else jnp.zeros_like(first), (1,))
        back = pl.pallas_call(
            columns_kernel,
            name="columns",
            grid=(wide // SUBLANES,),
            in_specs=[
                pl.BlockSpec(memory_space=pltpu.SMEM),
                pl.BlockSpec(memory_space=pltpu.SMEM),
                pl.BlockSpec((holders_all, 2, 2, SUBLANES, rows), lambda i: (0, 0, 0, i, 0)),
                pl.BlockSpec((SUBLANES, LANES), lambda i: (i, 0)),
                whole(matrix_shape),
                whole(matrix_shape),
                whole(table.shape),
            ],
            out_specs=pl.BlockSpec((holders_all, 2, SUBLANES, rows), lambda i: (0, 0, i, 0)),
            out_shape=jax.ShapeDtypeStruct((holders_all, 2, wide, rows), jnp.float32),
            scratch_shapes=[
                pltpu.VMEM((pieces * SUBLANES, 2 * LANES), jnp.float32),
                pltpu.VMEM((total_bins, pieces * SUBLANES, 2 * LANES), jnp.float32),
                pltpu.VMEM((pieces * SUBLANES, 2 * LANES), jnp.float32),
            ],
            compiler_params=limit,
        )(flag, masked, got, col_freq[chunk * wide : (chunk + 1) * wide], to_frequency, to_rows, table)
        returned.append(
            lax.all_to_all(back, ("bin", "tile"), split_axis=0, concat_axis=0, tiled=True)
            .reshape(blocks, holders, 2, wide, rows)
        )

    field = pl.pallas_call(
        back_kernel,
        name="rows_back",
        grid=(rows // step_rows,),
        in_specs=[
            pl.BlockSpec((blocks, holders, 2, wide, step_rows), lambda i: (0, 0, 0, 0, i))
        ] * CHUNKS + [whole(matrix_shape), whole(matrix_shape), whole(table.shape)],
        out_specs=pl.BlockSpec((step_rows, length), lambda i: (i, 0)),
        out_shape=jax.ShapeDtypeStruct((rows, length), jnp.float32),
        scratch_shapes=[pltpu.VMEM((blocks, step_rows, 2 * LANES), jnp.float32)],
        compiler_params=limit,
    )(*returned, inverse, edge_inverse, table)
    return field[None]


def solution(mesh):
    in_specs = (P("bin", "tile", None), P("bin", "tile", None), P())
    out_specs = P("bin", "tile", None)
    return jax.shard_map(
        on_device, mesh=mesh, in_specs=in_specs, out_specs=out_specs, check_vma=False
    )
```

time: 1330 us -> 632 us (0.48)
  matrix products: 553 us -> 0 us
  waiting for transfers between devices: 555 us -> 247 us
  blocking collectives: 0 us -> 288 us
  local copies, waits for them, and re-layouts: 181 us -> 1.43 us
  Pallas kernels: 0 us -> 84.4 us
    dot_general x32 -> x0, matrix products: 553 us -> none  [the longest x7 132 us: complex_einsum(): jnp.einsum(form, left_real, right_imag, precision=exact)]
    all_to_all x4 -> x2, waiting for transfers between devices: 555 us -> 247 us  [the longest x1 169 us: on_device(): lax.all_to_all(sent[chunk].reshape(holders_all, 2, 2, wide, rows), ('bin'...]
    all_to_all x0 -> x2, blocking collectives: none -> 288 us  [the longest x1 190 us: on_device(): lax.all_to_all(sent[chunk].reshape(holders_all, 2, 2, wide, rows), ('bin'...]
    pallas_call x0 -> x4, Pallas kernels: none -> 84.4 us  [the longest x1 33.1 us: on_device(): pl.pallas_call(rows_kernel, name='rows_forward', grid=(rows // step_rows,...]
    reshape x2 -> x0, local copies, waits for them, and re-layouts: 45.6 us -> none  [the longest x1 22.8 us: transform_last(): out_imag.reshape(batch, length, height)]
    all_to_all x4 -> x0, local copies, waits for them, and re-layouts: 35.8 us -> none  [the longest x1 8.96 us: on_device(): lax.all_to_all(ungroup(inverse_imag), ('bin', 'tile'), split_axis=2, conc...]
    unnamed x36 -> x2, local copies, waits for them, and re-layouts: 33.4 us -> 0.01 us
    add x3 -> x0, local copies, waits for them, and re-layouts: 24.9 us -> none  [complex_einsum(): jnp.einsum(form, left_real, right_imag, precision=exact)]
  transfers between devices with their start and end apart: 4 -> 2, of which waited for: 4 -> 2; matrix products, arithmetic and copies ran while one was open for 15% -> 0% of each run, Pallas kernels for 0% -> 5%
where the time goes in v1:
time: 632 us; the launch traced here: 629 us
  blocking collectives  288 us (46%)
  waiting for transfers between devices  247 us (39%)
  Pallas kernels  84.4 us (13%)
  starting transfers between devices  7.88 us (1%)
    all_to_all x1, blocking collectives, on_device(): lax.all_to_all(sent[chunk].reshape(holders_all, 2, 2, wide, rows), ('bin'...  190 us
    all_to_all x1, waiting for transfers between devices, on_device(): lax.all_to_all(sent[chunk].reshape(holders_all, 2, 2, wide, rows), ('bin'...  169 us
    all_to_all x1, blocking collectives, on_device(): lax.all_to_all(back, ('bin', 'tile'), split_axis=0, concat_axis=0, tiled=...  98.1 us
    all_to_all x1, waiting for transfers between devices, on_device(): lax.all_to_all(back, ('bin', 'tile'), split_axis=0, concat_axis=0, tiled=...  77.2 us
    pallas_call x1, Pallas kernels, on_device(): pl.pallas_call(rows_kernel, name='rows_forward', grid=(rows // step_rows,...  33.1 us
    pallas_call x2, Pallas kernels, on_device(): pl.pallas_call(columns_kernel, name='columns', grid=(wide // SUBLANES,),...  33.1 us
    pallas_call x1, Pallas kernels, on_device(): pl.pallas_call(back_kernel, name='rows_back', grid=(rows // step_rows,),...  18.1 us
  transfers between devices with their start and end apart: 2, of which 2 were waited for; matrix products, arithmetic and copies ran while one was open for 0% of the time, Pallas kernels for 5%

profile of v1, /device:TPU:3, one launch (start us, length us, event | category | flops | bytes accessed | tf_op | source)
XLA Modules:
  0.0 629.4 jit_solution(11756947320689376730)
XLA Ops:
  0.0 33.1 %rows_forward.1 = (f32[16,2,2,2,32,512]{5,4,3,2,1,0:T(8,128)}, f32[16,2,2,2,32,512]{5,4,3,2,1,0:T(8,128)}) custom-call(f32[512,4096]{1,0:T(8,128)} %bitcast.13, f32[512,4096]{1,0:T(8,128)} %bitcast.14, bf16[2,256,256]{2,1,0:T(8,128)(2,1)} %constant.70.clone.matrix_ref.refs_2_, bf16[2,256,256]{2,1,0:T(8,128)(2,1)} %constant.71.clone.edge_ref, ...), custom_call_target="tpu_custom_call" | custom-call | tf_op jit(solution)/shard_map/rows_forward/pallas_call | solution.py:400
  33.1 190.3 %all_to_all.20.in_ref = f32[32,2,2,32,512]{4,3,2,1,0:T(8,128)} all-to-all(f32[32,2,2,32,512]{4,3,2,1,0:T(8,128)} %bitcast.16), channel_id=1, replica_groups=mesh['bin'=4,'tile'=8] {'bin','tile'}, dimensions={0} | all-to-all | bytes 16777216 | tf_op jit(solution)/shard_map/all_to_all | solution.py:426
  223.5 0.0 copy-start
  223.5 4.6 all-to-all-start.2
  228.1 0.1 slice_bitcast_fusion
  228.2 0.0 copy-done
  228.2 0.6 fusion.weights_ref
  228.8 0.7 broadcast_in_dim.6.freq_ref
  229.4 16.5 %columns.2 = f32[32,2,32,512]{3,2,1,0:T(8,128)} custom-call(s32[1]{0:T(128)} %bitcast.flag_ref, f32[4,4]{1,0:T(4,128)} %fusion.weights_ref, f32[32,2,2,32,512]{4,3,2,1,0:T(8,128)} %all_to_all.20.in_ref, f32[32,128]{1,0:T(8,128)} %broadcast_in_dim.6.freq_ref, bf16[2,256,256]{2,1,0:T(8,128)(2,1)} %constant.73.clone.forward_ref, ...), custom_call_target="tpu_custom_call" | custom-call | tf_op jit(solution)/shard_map/columns/pallas_call | solution.py:431
  246.0 169.4 %all-to-all-done.2.in_ref = f32[32,2,2,32,512]{4,3,2,1,0:T(8,128)} async-done(((f32[32,2,2,32,512]{4,3,2,1,0:T(8,128)}), f32[32,2,2,32,512]{4,3,2,1,0:T(8,128)}, u32[]{:S(2)}, u32[]{:S(2)}) %all-to-all-start.2) | async-done | bytes 8388640 | tf_op jit(solution)/shard_map/all_to_all | solution.py:426
  415.4 3.3 all-to-all-start.1
  418.7 0.7 broadcast_in_dim.14.freq_ref
  419.4 16.6 %columns.3 = f32[32,2,32,512]{3,2,1,0:T(8,128)} custom-call(s32[1]{0:T(128)} %constant.69.clone.1.flag_ref, f32[4,4]{1,0:T(4,128)} %fusion.weights_ref, f32[32,2,2,32,512]{4,3,2,1,0:T(8,128)} %all-to-all-done.2.in_ref, f32[32,128]{1,0:T(8,128)} %broadcast_in_dim.14.freq_ref, bf16[2,256,256]{2,1,0:T(8,128)(2,1)} %constant.73.clone.forward_ref, ...), custom_call_target="tpu_custom_call" | custom-call | tf_op jit(solution)/shard_map/columns/pallas_call | solution.py:431
  436.0 77.2 %all-to-all-done.1 = f32[32,2,32,512]{3,2,1,0:T(8,128)} async-done(((f32[32,2,32,512]{3,2,1,0:T(8,128)}), f32[32,2,32,512]{3,2,1,0:T(8,128)}, u32[]{:S(2)}, u32[]{:S(2)}) %all-to-all-start.1) | async-done | bytes 4194336 | tf_op jit(solution)/shard_map/all_to_all | solution.py:454
  513.2 98.1 %all_to_all.21 = f32[32,2,32,512]{3,2,1,0:T(8,128)} all-to-all(f32[32,2,32,512]{3,2,1,0:T(8,128)} %columns.3), channel_id=1, replica_groups=mesh['bin'=4,'tile'=8] {'bin','tile'}, dimensions={0} | all-to-all | bytes 8388608 | tf_op jit(solution)/shard_map/all_to_all | solution.py:454
  611.3 18.1 %rows_back.1 = f32[512,4096]{1,0:T(8,128)} custom-call(f32[16,2,2,32,512]{4,3,2,1,0:T(8,128)} %bitcast.5.refs_0_, f32[16,2,2,32,512]{4,3,2,1,0:T(8,128)} %bitcast.12, bf16[2,256,256]{2,1,0:T(8,128)(2,1)} %constant.70.clone.matrix_ref.refs_2_, bf16[2,256,256]{2,1,0:T(8,128)(2,1)} %constant.75.clone.refs_3_, f32[2,32,8,128]{3,2,1,0:T(8,128)} %constant.72.clone.twiddle_ref.refs_4_), custom_call_target="tpu_custom_call" | custom-call | tf_op jit(solution)/shard_map/rows_back/pallas_call | solution.py:458
  (1 shorter events, 0.0 us)
Async XLA Ops:
  223.5 4.7 copy-start
  223.5 191.9 %all-to-all-start.2 = ((f32[32,2,2,32,512]{4,3,2,1,0:T(8,128)}), f32[32,2,2,32,512]{4,3,2,1,0:T(8,128)}, u32[]{:S(2)}, u32[]{:S(2)}) async-start(f32[32,2,2,32,512]{4,3,2,1,0:T(8,128)} %bitcast.15), calls=%async_computation.2 | async-start | bytes 16777216 | tf_op jit(solution)/shard_map/all_to_all | solution.py:426
  415.4 97.7 %all-to-all-start.1 = ((f32[32,2,32,512]{3,2,1,0:T(8,128)}), f32[32,2,32,512]{3,2,1,0:T(8,128)}, u32[]{:S(2)}, u32[]{:S(2)}) async-start(f32[32,2,32,512]{3,2,1,0:T(8,128)} %columns.2), calls=%async_computation.1 | async-start | bytes 8388608 | tf_op jit(solution)/shard_map/all_to_all | solution.py:454
